TPU v7x, 32 devices: a whole 2x2x4 slice. The times are simulated.
32 devices in a mesh: grp: 4 (over z), elem: 8 (over y, x, core).
Axes of the slice: x: 2, y: 2, z: 4, core: 2. Of those that a mesh axis runs over, the one named last changes fastest.
Arguments:
- velocity: float32 [3, 343, 4096], P(None, None, ('grp', 'elem')), may hold values from -0.6 to 0.6
- adjoint: float32 [3, 343, 4096], P(None, None, ('grp', 'elem')), may hold values from -0.6 to 0.6
- spacing: float32 [3, 4096], P(None, ('grp', 'elem')), may hold values from 0.5 to 2
- elem_count: int32 [32], P(('grp', 'elem')), may hold values from 32 to 128, as said below
- design_map: int32 [8, 4096], P(None, ('grp', 'elem')), may hold values from 0 to 65535, as said below
Outputs:
- direction: float32 [3, 65536], P(None, ('grp', 'elem'))
- objective: float32 [], replicated
Inputs may be any that keep to these rules, and one draw needn't show every extreme that they name: `elem_count`: the largest count equals 128 in every draw. `design_map`: design node d belongs to the device numbered d // 2048, counting grp first and elem second. Every entry of a device's columns names a node of a device whose elem index differs from that device's by at most one, cyclically over the elem axis, in any group.
All inputs are finite; a program needn't handle non-finite values.
Results may differ from a plain program's by a relative error of at most 0.0003.
Values sent between devices are 32-bit elements; how exact they have to be, the bound alone decides.
A program may use at most 64 MiB of HBM per device.

v0:
```python
import jax
import jax.numpy as jnp
import numpy as np
from jax import lax
from jax.sharding import PartitionSpec as P

P_SIZE = 7
ND_DEV = 2048


def passed_along(array, axis, by):
    devices = lax.axis_size(axis)
    return lax.ppermute(array, axis, [(i, (i + by) % devices) for i in range(devices)])


def lobatto(degree):
    points = np.cos(np.pi * np.arange(degree + 1) / degree)
    for sweep in range(60):
        lower = np.ones(degree + 1)
        upper = points.copy()
        for order in range(2, degree + 1):
            lower, upper = (upper, ((2 * order - 1) * points * upper - (order - 1) * lower) / order)
        points = points - (points * upper - lower) / ((degree + 1) * upper)
    lower = np.ones(degree + 1)
    upper = points.copy()
    for order in range(2, degree + 1):
        lower, upper = (upper, ((2 * order - 1) * points * upper - (order - 1) * lower) / order)
    return (points[::-1].copy(), upper[::-1].copy())


def tables():
    degree = P_SIZE - 1
    points, values = lobatto(degree)
    weights = 2.0 / (degree * (degree + 1) * values**2)
    derivative = np.zeros((P_SIZE, P_SIZE))
    for i in range(P_SIZE):
        for j in range(P_SIZE):
            if i != j:
                derivative[i, j] = values[i] / (values[j] * (points[i] - points[j]))
    derivative[0, 0] = -degree * (degree + 1) / 4.0
    derivative[P_SIZE - 1, P_SIZE - 1] = degree * (degree + 1) / 4.0
    coords = np.meshgrid(points, points, points, indexing="ij")
    coords = [c.reshape(-1) for c in coords]
    spread = np.meshgrid(weights, weights, weights, indexing="ij")
    quadrature = (spread[0] * spread[1] * spread[2]).reshape(-1)
    vertex_grad = np.zeros((3, 8, P_SIZE**3))
    for vertex in range(8):
        signs = [2.0 * (vertex >> 2 - m & 1) - 1.0 for m in range(3)]
        factors = [(1.0 + signs[m] * coords[m]) / 2.0 for m in range(3)]
        for j in range(3):
            others = [factors[m] for m in range(3) if m != j]
            vertex_grad[j, vertex] = signs[j] / 2.0 * others[0] * others[1] * quadrature
    unit = np.eye(P_SIZE)
    directional = np.stack(
        [
            np.kron(np.kron(derivative, unit), unit),
            np.kron(np.kron(unit, derivative), unit),
            np.kron(np.kron(unit, unit), derivative),
        ]
    )
    return (
        jnp.asarray(directional, jnp.float32),
        jnp.asarray(vertex_grad, jnp.float32),
        jnp.asarray(quadrature, jnp.float32),
    )


def element_terms(velocity, adjoint, spacing, directional, vertex_grad, quadrature):
    factor = 2.0 / spacing
    jacobian = spacing[0] * spacing[1] * spacing[2] / 8.0
    highest = lax.Precision.HIGHEST

    def gradient(field):
        return [
            [
                jnp.dot(directional[j], field[i], precision=highest) * factor[j][None, :]
                for j in range(3)
            ]
            for i in range(3)
        ]

    grad_u = gradient(velocity)
    grad_w = gradient(adjoint)
    inner = grad_u[0][0] * grad_w[0][0]
    squared = grad_u[0][0] * grad_u[0][0]
    for i in range(3):
        for k in range(3):
            if i + k > 0:
                inner = inner + grad_u[i][k] * grad_w[i][k]
                squared = squared + grad_u[i][k] * grad_u[i][k]
    cross = [
        [
            grad_u[0][c] * grad_w[0][j] + grad_u[1][c] * grad_w[1][j] + grad_u[2][c] * grad_w[2][j]
            for j in range(3)
        ]
        for c in range(3)
    ]
    rows = []
    for c in range(3):
        total = None
        for j in range(3):
            stress = -cross[c][j] - cross[j][c]
            if c == j:
                stress = stress + inner
            piece = jnp.dot(vertex_grad[j], stress, precision=highest) * factor[j][None, :]
            total = piece if total is None else total + piece
        rows.append(total * jacobian[None, :])
    terms = jnp.stack(rows)
    dissipated = jacobian * jnp.dot(quadrature, squared, precision=highest)
    return (terms, dissipated)


def body(velocity, adjoint, spacing, elem_count, design_map):
    slots = velocity.shape[-1]
    block = min(256, slots)
    groups = lax.axis_size("grp")
    columns = lax.axis_size("elem")
    design_total = ND_DEV * groups * columns
    directional, vertex_grad, quadrature = tables()
    extent = 3 * groups * ND_DEV
    home_col = lax.axis_index("elem")
    owner = design_map // ND_DEV
    offset = (owner % columns - home_col + 1 + columns) % columns
    target = (offset * groups + owner // columns) * ND_DEV + design_map % ND_DEV
    count = elem_count[0]
    live_blocks = (count + block - 1) // block

    def step(index, carry):
        assembled, spent = carry
        start = index * block
        terms, dissipated = element_terms(
            velocity, adjoint, spacing, directional, vertex_grad, quadrature
        )
        live = (start + jnp.arange(block, dtype=jnp.int32) < count).astype(jnp.float32)
        terms = terms * live[None, None, :]
        assembled = assembled.at[:, target.reshape(-1)].add(terms.reshape(3, -1))
        return (assembled, spent + jnp.sum(dissipated * live))

    init = (jnp.zeros((3, extent), jnp.float32), jnp.zeros((), jnp.float32))
    assembled, spent = lax.fori_loop(0, live_blocks, step, init)
    spent_total = lax.psum(spent, ("grp", "elem"))
    layered = assembled.reshape(3, 3, groups, ND_DEV)
    nearby = lax.psum_scatter(layered, "grp", scatter_dimension=2, tiled=True).reshape(3, 3, ND_DEV)
    from_above = passed_along(nearby[:, 0], "elem", -1)
    from_below = passed_along(nearby[:, 2], "elem", 1)
    gradient_sum = nearby[:, 1] + from_above + from_below
    squares = jnp.sum(gradient_sum * gradient_sum)
    square_total = lax.psum(squares, ("grp", "elem"))
    direction = gradient_sum * lax.rsqrt(square_total / (3.0 * design_total) + 1e-06)
    objective = spent_total / (P_SIZE**3 * slots * groups * columns)
    return (direction, objective)


def solution(mesh):
    return jax.shard_map(
        body,
        mesh=mesh,
        in_specs=(
            P(None, None, ("grp", "elem")),
            P(None, None, ("grp", "elem")),
            P(None, ("grp", "elem")),
            P(("grp", "elem")),
            P(None, ("grp", "elem")),
        ),
        out_specs=(P(None, ("grp", "elem")), P()),
        check_vma=False,
    )
```

profile of v0, /device:TPU:0, one launch (start us, length us, event | category | flops | bytes accessed | tf_op | source)
XLA Modules:
  0.0 169.3 jit_solution(300287576888361234)
XLA Ops:
  8.0 0.8 fusion.138
  8.8 0.8 slice_multiply_fusion
  9.6 0.7 broadcast_divide_fusion.1
  10.3 1.8 %convolution_multiply_fusion.15 = f32[343,128]{1,0:T(8,128)S(1)} fusion(f32[343,343]{1,0:T(8,128)} %constant.151, f32[3,343,128]{2,1,0:T(8,128)} %param.10, f32[128]{0:T(128)S(1)} %get-tuple-element.464), kind=kOutput, calls=%fused_computation.32 | convolution fusion | flops 180752768 | bytes 880640 | tf_op jit(solution)/shard_map/while/body/dot_general | solution.py:76
  12.1 1.8 %convolution_multiply_fusion.13 = f32[343,128]{1,0:T(8,128)S(1)} fusion(f32[343,343]{1,0:T(8,128)} %constant.151, f32[3,343,128]{2,1,0:T(8,128)} %param.10, f32[128]{0:T(128)S(1)} %get-tuple-element.464), kind=kOutput, calls=%fused_computation.30 | convolution fusion | flops 180752768 | bytes 880640 | tf_op jit(solution)/shard_map/while/body/dot_general | solution.py:76
  13.9 1.8 %convolution_multiply_fusion.17 = f32[343,128]{1,0:T(8,128)S(1)} fusion(f32[343,343]{1,0:T(8,128)} %constant.151, f32[3,343,128]{2,1,0:T(8,128)} %param.10, f32[128]{0:T(128)S(1)} %get-tuple-element.464), kind=kOutput, calls=%fused_computation.34 | convolution fusion | flops 180752768 | bytes 880640 | tf_op jit(solution)/shard_map/while/body/dot_general | solution.py:76
  15.7 1.8 %convolution_multiply_fusion.5 = f32[343,128]{1,0:T(8,128)S(1)} fusion(f32[343,343]{1,0:T(8,128)} %constant.155, f32[3,343,128]{2,1,0:T(8,128)} %param.10, f32[128]{0:T(128)S(1)} %get-tuple-element.465), kind=kOutput, calls=%fused_computation.22 | convolution fusion | flops 180752768 | bytes 880640 | tf_op jit(solution)/shard_map/while/body/dot_general | solution.py:76
  17.5 1.8 %convolution_multiply_fusion.1 = f32[343,128]{1,0:T(8,128)S(1)} fusion(f32[343,343]{1,0:T(8,128)} %constant.155, f32[3,343,128]{2,1,0:T(8,128)} %param.10, f32[128]{0:T(128)S(1)} %get-tuple-element.465), kind=kOutput, calls=%fused_computation.18 | convolution fusion | flops 180752768 | bytes 880640 | tf_op jit(solution)/shard_map/while/body/dot_general | solution.py:76
  19.2 1.8 %convolution_multiply_fusion.9 = f32[343,128]{1,0:T(8,128)S(1)} fusion(f32[343,343]{1,0:T(8,128)} %constant.155, f32[3,343,128]{2,1,0:T(8,128)} %param.10, f32[128]{0:T(128)S(1)} %get-tuple-element.465), kind=kOutput, calls=%fused_computation.26 | convolution fusion | flops 180752768 | bytes 880640 | tf_op jit(solution)/shard_map/while/body/dot_general | solution.py:76
  21.0 1.8 %convolution_multiply_fusion.7 = f32[343,128]{1,0:T(8,128)S(1)} fusion(f32[343,343]{1,0:T(8,128)} %constant.153, f32[3,343,128]{2,1,0:T(8,128)} %param.10, f32[128]{0:T(128)S(1)} %get-tuple-element.466), kind=kOutput, calls=%fused_computation.24 | convolution fusion | flops 180752768 | bytes 880640 | tf_op jit(solution)/shard_map/while/body/dot_general | solution.py:76
  22.8 1.8 %convolution_multiply_fusion.11 = f32[343,128]{1,0:T(8,128)S(1)} fusion(f32[343,343]{1,0:T(8,128)} %constant.153, f32[3,343,128]{2,1,0:T(8,128)} %param.10, f32[128]{0:T(128)S(1)} %get-tuple-element.466), kind=kOutput, calls=%fused_computation.28 | convolution fusion | flops 180752768 | bytes 880640 | tf_op jit(solution)/shard_map/while/body/dot_general | solution.py:76
  24.6 1.8 %convolution_multiply_fusion.16 = f32[343,128]{1,0:T(8,128)S(1)} fusion(f32[343,343]{1,0:T(8,128)} %constant.151, f32[3,343,128]{2,1,0:T(8,128)} %param.11, f32[128]{0:T(128)S(1)} %get-tuple-element.464), kind=kOutput, calls=%fused_computation.33 | convolution fusion | flops 180752768 | bytes 880640 | tf_op jit(solution)/shard_map/while/body/dot_general | solution.py:76
  26.4 1.8 %convolution_multiply_fusion.14 = f32[343,128]{1,0:T(8,128)S(1)} fusion(f32[343,343]{1,0:T(8,128)} %constant.151, f32[3,343,128]{2,1,0:T(8,128)} %param.11, f32[128]{0:T(128)S(1)} %get-tuple-element.464), kind=kOutput, calls=%fused_computation.31 | convolution fusion | flops 180752768 | bytes 880640 | tf_op jit(solution)/shard_map/while/body/dot_general | solution.py:76
  28.2 1.8 %convolution_multiply_fusion.12 = f32[343,128]{1,0:T(8,128)S(1)} fusion(f32[343,343]{1,0:T(8,128)} %constant.151, f32[3,343,128]{2,1,0:T(8,128)} %param.11, f32[128]{0:T(128)S(1)} %get-tuple-element.464), kind=kOutput, calls=%fused_computation.29 | convolution fusion | flops 180752768 | bytes 880640 | tf_op jit(solution)/shard_map/while/body/dot_general | solution.py:76
  29.9 1.8 %convolution_multiply_fusion.8 = f32[343,128]{1,0:T(8,128)S(1)} fusion(f32[343,343]{1,0:T(8,128)} %constant.155, f32[3,343,128]{2,1,0:T(8,128)} %param.11, f32[128]{0:T(128)S(1)} %get-tuple-element.465), kind=kOutput, calls=%fused_computation.25 | convolution fusion | flops 180752768 | bytes 880640 | tf_op jit(solution)/shard_map/while/body/dot_general | solution.py:76
  31.7 1.8 %convolution_multiply_fusion.4 = f32[343,128]{1,0:T(8,128)S(1)} fusion(f32[343,343]{1,0:T(8,128)} %constant.155, f32[3,343,128]{2,1,0:T(8,128)} %param.11, f32[128]{0:T(128)S(1)} %get-tuple-element.465), kind=kOutput, calls=%fused_computation.21 | convolution fusion | flops 180752768 | bytes 880640 | tf_op jit(solution)/shard_map/while/body/dot_general | solution.py:76
  33.5 1.8 %convolution_multiply_fusion = f32[343,128]{1,0:T(8,128)S(1)} fusion(f32[343,343]{1,0:T(8,128)} %constant.155, f32[3,343,128]{2,1,0:T(8,128)} %param.11, f32[128]{0:T(128)S(1)} %get-tuple-element.465), kind=kOutput, calls=%fused_computation.17 | convolution fusion | flops 180752768 | bytes 880640 | tf_op jit(solution)/shard_map/while/body/dot_general | solution.py:76
  35.3 1.6 convolution_multiply_fusion.10
  36.9 0.7 convolution_multiply_fusion.6
  37.6 0.9 convolution_multiply_fusion.2
  38.6 1.8 %multiply_add_fusion.1 = (f32[343,128]{1,0:T(8,128)S(1)}, f32[343,128]{1,0:T(8,128)S(1)}, f32[343,128]{1,0:T(8,128)S(1)}, f32[343,128]{1,0:T(8,128)S(1)}, f32[34...) fusion(f32[343,128]{1,0:T(8,128)S(1)} %convolution_multiply_fusion, ...), kind=kOutput, calls=%fused_computation.92 | convolution fusion | flops 182816256 | bytes 5037636 | tf_op jit(solution)/shard_map/while/body/dot_general | solution.py:76
  43.2 4.8 %broadcast_in_dim.2 = f32[3,24576]{0,1:T(8,128)} broadcast(f32[]{:T(128)} %copy.63), dimensions={} | broadcast | bytes 294916 | tf_op jit(solution)/shard_map/broadcast_in_dim | solution.py:139
  48.0 17.4 %while.16 = (s32[]{:T(128)}, f32[3,24576]{0,1:T(8,128)}, f32[]{:T(128)}, s32[]{:T(128)}, s32[8,128]{1,0:T(8,128)S(1)}, /*index=5*/f32[3,128]{1,0:T(4,128)S(1)}, ...) while((s32[]{:T(128)}, f32[3,24576]{0,1:T(8,128)}, ...), condition=%wide.region_3.4_spmd, body=%wide.region_0.3_spmd.sunk | while | flops 35459 | bytes 167145 | solution.py:140
  48.0 1.3 fusion.142
  49.9 0.7 compare_convert_fusion.2
  50.9 14.5 %scatter_fusion = f32[3,24576]{0,1:T(8,128)} fusion(f32[3,24576]{0,1:T(8,128)} %get-tuple-element.620, s32[1024]{0:T(1024)S(1)} %bitcast.148, f32[1024,3]{1,0:T(8,128)S(1)} %copy.47), kind=kCustom, calls=%fused_computation.clone.1 | custom fusion | flops 3072 | bytes 40960 | tf_op jit(solution)/shard_map/while/body/scatter-add | solution.py:136
  65.4 8.3 %copy.23 = f32[3,3,4,2048]{3,2,1,0:T(4,128)} copy(f32[3,3,4,2048]{0,3,2,1:T(8,128)} %bitcast.147) | data formatting | bytes 589824 | tf_op jit(solution)/shard_map/reshape | solution.py:142
  74.3 38.2 %all-reduce.4.cloned.1.call-done = f32[3,3,4,2048]{3,2,1,0:T(4,128)} async-done(((f32[3,3,4,2048]{3,2,1,0:T(4,128)}), f32[3,3,4,2048]{3,2,1,0:T(4,128)}) %all-reduce.4.cloned.1.call-update) | async-done | bytes 294928
  112.6 1.7 constant_dynamic-slice_fusion
  115.0 1.1 collective-permute-done
  116.1 3.0 %collective-permute-done.1 = f32[3,2048]{1,0:T(4,128)S(1)} collective-permute-done((f32[3,2048]{1,0:T(4,128)S(1)}, f32[3,2048]{1,0:T(4,128)S(1)}, u32[]{:S(2)}, u32[]{:S(2)}) %collective-permute-start.1) | collective-permute-done | bytes 24608 | tf_op jit(solution)/shard_map/ppermute | solution.py:13
  119.7 39.6 %all-reduce.1 = (f32[]{:T(128)}, f32[]{:T(128)}) all-reduce(f32[]{:T(128)} %multiply_reduce_fusion, f32[]{:T(128)} %get-tuple-element.406), channel_id=1, replica_groups=mesh['grp'=4,'elem'=8] {'grp','elem'}, use_global_device_ids=true, to_apply=%region_6.7 | all-reduce | flops 2 | bytes 16 | tf_op jit(solution)/shard_map/psum | solution.py:148
  (48 shorter events, 5.6 us)
Async XLA Ops:
  7.2 28.1 %copy-start = (f32[343,343]{1,0:T(8,128)S(1)}, f32[343,343]{1,0:T(8,128)}, u32[]{:S(2)}) copy-start(f32[343,343]{1,0:T(8,128)} %constant.153) | copy-start | bytes 1411792
  7.2 33.2 %copy-start.5 = (f32[8,343]{1,0:T(8,128)S(1)}, f32[8,343]{1,0:T(8,128)}, u32[]{:S(2)}) copy-start(f32[8,343]{1,0:T(8,128)} %constant.161) | copy-start | bytes 32932
  7.2 33.5 %copy-start.4 = (f32[8,343]{1,0:T(8,128)S(1)}, f32[8,343]{1,0:T(8,128)}, u32[]{:S(2)}) copy-start(f32[8,343]{1,0:T(8,128)} %constant.157) | copy-start | bytes 32932
  7.2 34.5 %copy-start.3 = (f32[8,343]{1,0:T(8,128)S(1)}, f32[8,343]{1,0:T(8,128)}, u32[]{:S(2)}) copy-start(f32[8,343]{1,0:T(8,128)} %constant.159) | copy-start | bytes 32932
  7.2 29.7 %copy-start.1 = (f32[3,343,128]{2,1,0:T(8,128)S(1)}, f32[3,343,128]{2,1,0:T(8,128)}, u32[]{:S(2)}) copy-start(f32[3,343,128]{2,1,0:T(8,128)} %param.11) | copy-start | bytes 1580548
  7.2 105.3 %all-reduce.4.cloned.1.call-start = ((), (), s32[]{:S(2)}) async-start(), calls=%async_computation | async-start | bytes 589824
  12.1 30.7 %copy-start.7 = (f32[343,1]{0,1:T(1,128)S(1)}, f32[343,1]{0,1:T(1,128)}, u32[]{:S(2)}) copy-start(f32[343,1]{0,1:T(1,128)} %constant.166) | copy-start | bytes 4120
  15.7 27.5 %copy-start.6 = (s32[8,128]{1,0:T(8,128)S(1)}, s32[8,128]{1,0:T(8,128)}, u32[]{:S(2)}) copy-start(s32[8,128]{1,0:T(8,128)} %param.14) | copy-start | bytes 12292
  38.5 9.4 %copy-start.2 = (f32[3,128]{1,0:T(4,128)S(1)}, f32[3,128]{1,0:T(4,128)}, u32[]{:S(2)}) copy-start(f32[3,128]{1,0:T(4,128)} %param.12) | copy-start | bytes 4612
  43.2 30.6 %copy-start.8 = (u32[32]{0:T(128)S(1)}, u32[32]{0:T(128)}, u32[]{:S(2)}) copy-start(u32[32]{0:T(128)} %constant.164) | copy-start | bytes 388
  114.4 1.7 collective-permute-start
  114.5 4.6 %collective-permute-start.1 = (f32[3,2048]{1,0:T(4,128)S(1)}, f32[3,2048]{1,0:T(4,128)S(1)}, u32[]{:S(2)}, u32[]{:S(2)}) collective-permute-start(f32[3,2048]{1,0:T(4,128)S(1)} %bitcast.154), channel_id=1, source_target_pairs={{0,1},{1,2},{2,3},{3,4},{4,5},{5,6},{6,7},{7,0},{8,9},{9,10},{10,1... | collective-permute-start | bytes 73736 | tf_op jit(solution)/shard_map/ppermute | solution.py:13
Sparse Core Ops, SparseCore 0:
  73.8 38.6 all-reduce.3
where the time goes:
time: 170 us; the launch traced here: 169 us
  waiting for transfers between devices  42.4 us (25%)
  blocking collectives  39.6 us (23%)
  matrix products  32.6 us (19%)
  other arithmetic  20.1 us (12%)
  between operations  17.5 us (10%)
  local copies, waits for them, and re-layouts  15.8 us (9%)
    psum x1, blocking collectives, body(): square_total = lax.psum(squares, ('grp', 'elem'))  39.6 us
    unnamed x2, waiting for transfers between devices  38.2 us
    dot_general x18, matrix products, gradient(): jnp.dot(directional[j], field[i], precision=highest) * factor[j][None, :]  30 us
    scatter-add x1, other arithmetic, step(): assembled = assembled.at[:, target.reshape(-1)].add(terms.reshape(3, -1))  14.5 us
    reshape x1, local copies, waits for them, and re-layouts, body(): layered = assembled.reshape(3, 3, groups, ND_DEV)  8.27 us
    broadcast_in_dim x1, local copies, waits for them, and re-layouts, body(): init = (jnp.zeros((3, extent), jnp.float32), jnp.zeros((), jnp.float32))  4.81 us
    ppermute x2, waiting for transfers between devices, passed_along(): lax.ppermute(array, axis, [(i, (i + by) % devices) for i in range(devices)])  4.11 us
  transfers between devices with their start and end apart: 3, of which 3 were waited for; matrix products, arithmetic and copies ran while one was open for 0% of the time, Pallas kernels for 0%

commit v1 on v0

v1 whole, which is shorter than its diff:
```python
import functools

import jax
import jax.numpy as jnp
import numpy as np
from jax import lax
from jax.experimental import pallas as pl
from jax.experimental.pallas import tpu as pltpu
from jax.sharding import PartitionSpec as P

P_SIZE = 7
ND_DEV = 2048
LANES = 128
LOW = 256
NODES = P_SIZE**3
ROWS = -(-NODES // 16) * 16
MESH = pl.DeviceIdType.MESH
F32 = jnp.float32
BF16 = jnp.bfloat16


def lobatto(degree):
    points = np.cos(np.pi * np.arange(degree + 1) / degree)
    for sweep in range(60):
        lower = np.ones(degree + 1)
        upper = points.copy()
        for order in range(2, degree + 1):
            lower, upper = (upper, ((2 * order - 1) * points * upper - (order - 1) * lower) / order)
        points = points - (points * upper - lower) / ((degree + 1) * upper)
    lower = np.ones(degree + 1)
    upper = points.copy()
    for order in range(2, degree + 1):
        lower, upper = (upper, ((2 * order - 1) * points * upper - (order - 1) * lower) / order)
    return (points[::-1].copy(), upper[::-1].copy())


def halves(table):
    exact = np.asarray(table, np.float32)
    high = exact.astype(BF16)
    low = (exact - high.astype(np.float32)).astype(BF16)
    return (high, low)


def tables():
    degree = P_SIZE - 1
    points, values = lobatto(degree)
    weights = 2.0 / (degree * (degree + 1) * values**2)
    derivative = np.zeros((P_SIZE, P_SIZE))
    for i in range(P_SIZE):
        for j in range(P_SIZE):
            if i != j:
                derivative[i, j] = values[i] / (values[j] * (points[i] - points[j]))
    derivative[0, 0] = -degree * (degree + 1) / 4.0
    derivative[P_SIZE - 1, P_SIZE - 1] = degree * (degree + 1) / 4.0
    coords = np.meshgrid(points, points, points, indexing="ij")
    coords = [c.reshape(-1) for c in coords]
    spread = np.meshgrid(weights, weights, weights, indexing="ij")
    quadrature = (spread[0] * spread[1] * spread[2]).reshape(-1)
    contract = np.zeros((32, ROWS))
    for vertex in range(8):
        signs = [2.0 * (vertex >> 2 - m & 1) - 1.0 for m in range(3)]
        factors = [(1.0 + signs[m] * coords[m]) / 2.0 for m in range(3)]
        for j in range(3):
            others = [factors[m] for m in range(3) if m != j]
            contract[8 * j + vertex, :NODES] = signs[j] / 2.0 * others[0] * others[1] * quadrature
    contract[24, :NODES] = quadrature
    unit = np.eye(P_SIZE)
    directional = np.zeros((3, ROWS, NODES))
    directional[0, :NODES] = np.kron(np.kron(derivative, unit), unit)
    directional[1, :NODES] = np.kron(np.kron(unit, derivative), unit)
    directional[2, :NODES] = np.kron(np.kron(unit, unit), derivative)
    return (
        *halves(directional.reshape(3 * ROWS, NODES)),
        np.concatenate(halves(contract)),
    )


def split(value):
    high = value.astype(BF16)
    return (high, (value - high.astype(F32)).astype(BF16))


def quotient(value, by):
    if by & (by - 1) == 0:
        return lax.shift_right_logical(value, jnp.full_like(value, by.bit_length() - 1))
    return lax.div(value, jnp.full_like(value, by))


def remainder(value, by):
    if by & (by - 1) == 0:
        return value & (by - 1)
    return lax.rem(value, jnp.full_like(value, by))


def element_terms(fields, spacing, live, high, low, contract):
    slots = spacing.shape[1]
    field_high, field_low = split(fields)
    grads = (
        jnp.dot(high, field_high, preferred_element_type=F32)
        + jnp.dot(low, field_high, preferred_element_type=F32)
        + jnp.dot(high, field_low, preferred_element_type=F32)
    )

    def grad(field, i, j):
        column = (3 * field + i) * slots
        return grads[j * ROWS : (j + 1) * ROWS, column : column + slots]

    def product(c, j):
        return sum(grad(0, i, c) * grad(1, i, j) for i in range(3))

    pairs = [(0, 1), (0, 2), (1, 2)]
    stack = [product(m, m) for m in range(3)]
    stack += [product(c, j) + product(j, c) for c, j in pairs]
    stack += [sum(grad(0, i, j) * grad(0, i, j) for i in range(3)) for j in range(3)]
    stack_high, stack_low = split(jnp.concatenate(stack, axis=1))
    both = jnp.dot(contract, stack_high, preferred_element_type=F32)
    sums = both[:32] + both[32:] + jnp.dot(contract[:32], stack_low, preferred_element_type=F32)

    def part(j, column):
        return sums[8 * j : 8 * j + 8, column * slots : (column + 1) * slots]

    factor = [2.0 / spacing[j : j + 1] for j in range(3)]
    square = [f * f for f in factor]
    jacobian = spacing[0:1] * spacing[1:2] * spacing[2:3] * 0.125
    terms = []
    for c in range(3):
        total = sum(square[m] * part(c, m) for m in range(3)) - 2.0 * square[c] * part(c, c)
        for column, pair in enumerate(pairs):
            if c in pair:
                j = pair[0] + pair[1] - c
                total = total - square[j] * part(j, 3 + column)
        terms.append(jnp.where(live, total * (factor[c] * jacobian), 0.0))
    spent = sum(square[j] * part(3, 6 + j) for j in range(3)) * jacobian
    return (terms, jnp.where(live, spent, 0.0))


def assemble(terms, target, blocks):
    upper = quotient(target, LOW)
    lower = remainder(target, LOW)
    slots = target.shape[1]
    rows = blocks * (ND_DEV // LOW)
    row_index = lax.broadcasted_iota(jnp.int32, (rows, slots), 0)
    low_index = lax.broadcasted_iota(jnp.int32, (LOW, slots), 0)
    parts = []
    for term in terms:
        high = term.astype(BF16).astype(F32)
        parts.append(high)
    for c in range(3):
        parts.append(terms[c] - parts[c])
    left = []
    right = []
    for k in range(8):
        hit = row_index == upper[k : k + 1]
        left.append(
            jnp.concatenate([jnp.where(hit, p[k : k + 1], 0.0).astype(BF16) for p in parts], axis=0)
        )
        right.append(jnp.where(low_index == lower[k : k + 1], 1.0, 0.0).astype(BF16))
    sums = lax.dot_general(
        jnp.concatenate(left, axis=1),
        jnp.concatenate(right, axis=1),
        (((1,), (1,)), ((), ())),
        preferred_element_type=F32,
    )
    return [sums[c * rows : (c + 1) * rows] + sums[(3 + c) * rows : (4 + c) * rows] for c in range(3)]


def kernel(
    groups, columns,
    velocity, adjoint, spacing, count, design_map, high, low, contract,
    direction, objective,
    outgoing, arrived, gathered, send_sem, recv_sem, send_all, recv_all,
):
    devices = groups * columns
    grp, col = lax.axis_index("grp"), lax.axis_index("elem")
    me = grp * columns + col
    slots = spacing.shape[1]

    barrier = pltpu.get_barrier_semaphore()

    def coords(step):
        peer = lax.rem(me + step, devices)
        return (peer // columns, lax.rem(peer, columns))

    def greet(step, carry):
        pl.semaphore_signal(barrier, inc=1, device_id=coords(step), device_id_type=MESH)
        return carry

    lax.fori_loop(1, devices, greet, 0)

    live = lax.broadcasted_iota(jnp.int32, (8, slots), 1) < count[0]
    fields = jnp.concatenate([f[i] for f in (velocity, adjoint) for i in range(3)], axis=1)
    terms, spent = element_terms(fields, spacing[...], live, high[...], low[...], contract[...])
    node = design_map[...]
    owner = quotient(node, ND_DEV)
    offset = remainder(remainder(owner, columns) - col + (1 + columns), columns)
    block = offset * groups + quotient(owner, columns)
    sums = assemble(terms, block * ND_DEV + remainder(node, ND_DEV), 3 * groups)
    for b in range(3 * groups):
        for c in range(3):
            outgoing[b, 8 * c : 8 * c + 8, :] = sums[c][8 * b : 8 * b + 8]

    pl.semaphore_wait(barrier, devices - 1)

    copies = []
    for step in [*range(groups // 2, groups), *range(groups // 2)]:
        for o in range(3):
            if step == 0 and o == 1:
                continue
            to_grp = lax.rem(grp + step, groups)
            slot = o * groups + step
            copy = pltpu.make_async_remote_copy(
                src_ref=outgoing.at[o * groups + to_grp],
                dst_ref=arrived.at[slot],
                send_sem=send_sem.at[slot],
                recv_sem=recv_sem.at[slot],
                device_id=(to_grp, lax.rem(col + (o - 1 + columns), columns)),
                device_id_type=MESH,
            )
            copy.start()
            copies.append((slot, copy))
    total = outgoing[groups + grp]
    for slot, copy in copies[::-1]:
        copy.wait_recv()
        total = total + arrived[slot]

    squares = total * total
    squares = squares[0:8] + squares[8:16] + squares[16:24]
    squares = squares[:, :LANES] + squares[:, LANES:]
    lane = lax.broadcasted_iota(jnp.int32, (8, LANES), 1)
    mixed = jnp.where(
        lane < LANES // 2,
        squares + pltpu.roll(squares, LANES // 2, 1),
        spent + pltpu.roll(spent, LANES // 2, 1),
    )
    gathered[me] = jnp.sum(mixed, axis=0, keepdims=True)

    def share(step):
        return pltpu.make_async_remote_copy(
            src_ref=gathered.at[me],
            dst_ref=gathered.at[me],
            send_sem=send_all.at[step],
            recv_sem=recv_all.at[step],
            device_id=coords(step),
            device_id_type=MESH,
        )

    def send(step, carry):
        share(step).start()
        return carry

    def receive(step, carry):
        share(step).wait_recv()
        return carry

    def finish(step, carry):
        share(step).wait_send()
        return carry

    lax.fori_loop(1, devices, send, 0)
    for slot, copy in copies:
        copy.wait_send()
    lax.fori_loop(1, devices, receive, 0)
    everything = jnp.sum(gathered[...], axis=0)
    first = lax.broadcasted_iota(jnp.int32, (1, LANES), 1) < LANES // 2
    square_total = jnp.sum(jnp.where(first, everything, 0.0), axis=1, keepdims=True)
    spent_total = jnp.sum(jnp.where(first, 0.0, everything), axis=1, keepdims=True)
    scale = lax.rsqrt(square_total * (1.0 / (3.0 * ND_DEV * devices)) + 1e-06)
    scaled = total * scale
    for c in range(3):
        direction[c] = scaled[8 * c : 8 * c + 8]
    objective[...] = spent_total * (1.0 / (NODES * slots * devices))
    lax.fori_loop(1, devices, finish, 0)


def body(groups, columns, velocity, adjoint, spacing, elem_count, design_map):
    devices = groups * columns
    blocks = 3 * groups
    vmem = pl.BlockSpec(memory_space=pltpu.VMEM)
    direction, objective = pl.pallas_call(
        functools.partial(kernel, groups, columns),
        out_shape=(
            jax.ShapeDtypeStruct((3, ND_DEV // LOW, LOW), F32),
            jax.ShapeDtypeStruct((1, 1), F32),
        ),
        in_specs=[vmem, vmem, vmem, pl.BlockSpec(memory_space=pltpu.SMEM), vmem, vmem, vmem, vmem],
        out_specs=(vmem, vmem),
        scratch_shapes=[
            pltpu.VMEM((blocks, 24, LOW), F32),
            pltpu.VMEM((blocks, 24, LOW), F32),
            pltpu.VMEM((devices, 1, LANES), F32),
            pltpu.SemaphoreType.DMA((blocks,)),
            pltpu.SemaphoreType.DMA((blocks,)),
            pltpu.SemaphoreType.DMA((devices,)),
            pltpu.SemaphoreType.DMA((devices,)),
        ],
        compiler_params=pltpu.CompilerParams(collective_id=0, has_side_effects=True),
    )(velocity, adjoint, spacing, elem_count, design_map, *tables())
    return (direction.reshape(3, ND_DEV), objective.reshape(()))


def solution(mesh):
    return jax.shard_map(
        functools.partial(body, mesh.shape["grp"], mesh.shape["elem"]),
        mesh=mesh,
        in_specs=(
            P(None, None, ("grp", "elem")),
            P(None, None, ("grp", "elem")),
            P(None, ("grp", "elem")),
            P(("grp", "elem")),
            P(None, ("grp", "elem")),
        ),
        out_specs=(P(None, ("grp", "elem")), P()),
        check_vma=False,
    )
```

time: 170 us -> 28 us (0.16)
  waiting for transfers between devices: 42.4 us -> 0 us
  blocking collectives: 39.6 us -> 0 us
  matrix products: 32.6 us -> 0 us
  Pallas kernels: 0 us -> 23.3 us
  other arithmetic: 20.1 us -> 0 us
  between operations: 17.5 us -> 3.05 us
  local copies, waits for them, and re-layouts: 15.8 us -> 1.37 us
    psum x1 -> x0, blocking collectives: 39.6 us -> none  [body(): square_total = lax.psum(squares, ('grp', 'elem'))]
    unnamed x2 -> x0, waiting for transfers between devices: 38.2 us -> none
    dot_general x28 -> x0, matrix products: 32.6 us -> none  [the longest x18 30 us: gradient(): jnp.dot(directional[j], field[i], precision=highest) * factor[j][None, :]]
    pallas_call x0 -> x1, Pallas kernels: none -> 23.3 us  [body(): pl.pallas_call(functools.partial(kernel, groups, columns), out_shape=(jax...]
    scatter-add x1 -> x0, other arithmetic: 14.5 us -> none  [step(): assembled = assembled.at[:, target.reshape(-1)].add(terms.reshape(3, -1))]
    reshape x1 -> x0, local copies, waits for them, and re-layouts: 8.27 us -> none  [body(): layered = assembled.reshape(3, 3, groups, ND_DEV)]
    broadcast_in_dim x1 -> x0, local copies, waits for them, and re-layouts: 4.81 us -> none  [body(): init = (jnp.zeros((3, extent), jnp.float32), jnp.zeros((), jnp.float32))]
    ppermute x2 -> x0, waiting for transfers between devices: 4.11 us -> none  [passed_along(): lax.ppermute(array, axis, [(i, (i + by) % devices) for i in range(devices)])]
  transfers between devices with their start and end apart: 3 -> 0, of which waited for: 3 -> 0; matrix products, arithmetic and copies ran while one was open for 0% -> 0% of each run, Pallas kernels for 0% -> 0%
where the time goes in v1:
time: 28 us; the launch traced here: 27.7 us
  Pallas kernels  23.3 us (83%)
  between operations  3.05 us (11%)
  local copies, waits for them, and re-layouts  1.37 us (5%)
    pallas_call x1, Pallas kernels, body(): pl.pallas_call(functools.partial(kernel, groups, columns), out_shape=(jax...  23.3 us
    unnamed x1, local copies, waits for them, and re-layouts  1.37 us

profile of v1, /device:TPU:0, one launch (start us, length us, event | category | flops | bytes accessed | tf_op | source)
XLA Modules:
  0.0 27.7 jit_solution(15257152225973750998)
XLA Ops:
  1.3 23.3 %shard_map.95 = (f32[3,8,256]{2,1,0:T(8,128)}, f32[1,1]{1,0:T(1,128)}) custom-call(f32[3,343,128]{2,1,0:T(8,128)} %velocity.1, f32[3,343,128]{2,1,0:T(8,128)} %adjoint.1, f32[3,128]{1,0:T(4,128)} %spacing.1, s32[1]{0:T(128)S(6)} %copy.12.count, s32[8,128]{1,0:T(8,128)} %design_map.1, bf16[1056,343]{1,0:T(8,128)(2,1)} %constant.6.clone.high, ...), custom_call_target="tpu_custom_call" | custom-call | tf_op jit(solution)/shard_map/pallas_call | solution.py:279
  24.6 1.4 %copy.10 = f32[1,3,8,256]{3,1,2,0:T(4,128)} copy(f32[1,3,8,256]{3,2,1,0:T(8,128)} %bitcast.4) | data formatting | bytes 49152

commit v2 on v1

--- a/solution.py
+++ b/solution.py
@@ -11,9 +11,12 @@
 P_SIZE = 7
 ND_DEV = 2048
 LANES = 128
-LOW = 256
+UPPER = ND_DEV // LANES
 NODES = P_SIZE**3
 ROWS = -(-NODES // 16) * 16
+HEAD = 240
+BACK = 192
+TAIL = ROWS - HEAD
 MESH = pl.DeviceIdType.MESH
 F32 = jnp.float32
 BF16 = jnp.bfloat16
@@ -69,8 +72,11 @@
     directional[0, :NODES] = np.kron(np.kron(derivative, unit), unit)
     directional[1, :NODES] = np.kron(np.kron(unit, derivative), unit)
     directional[2, :NODES] = np.kron(np.kron(unit, unit), derivative)
+    near = directional[1:]
     return (
-        *halves(directional.reshape(3 * ROWS, NODES)),
+        np.stack(halves(directional[0])),
+        np.stack(halves(near[:, :HEAD, :256].reshape(2 * HEAD, 256))),
+        np.stack(halves(near[:, HEAD:, BACK:].reshape(2 * TAIL, NODES - BACK))),
         np.concatenate(halves(contract)),
     )
 
@@ -80,30 +86,32 @@
     return (high, (value - high.astype(F32)).astype(BF16))
 
 
-def quotient(value, by):
-    if by & (by - 1) == 0:
-        return lax.shift_right_logical(value, jnp.full_like(value, by.bit_length() - 1))
-    return lax.div(value, jnp.full_like(value, by))
-
-
-def remainder(value, by):
-    if by & (by - 1) == 0:
-        return value & (by - 1)
-    return lax.rem(value, jnp.full_like(value, by))
-
-
-def element_terms(fields, spacing, live, high, low, contract):
+def derivatives(fields, far, head, tail):
+    high, low = split(fields)
+
+    def apply(table, begin, end):
+        return (
+            jnp.dot(table[0], high[begin:end], preferred_element_type=F32)
+            + jnp.dot(table[1], high[begin:end], preferred_element_type=F32)
+            + jnp.dot(table[0], low[begin:end], preferred_element_type=F32)
+        )
+
+    first = apply(far, 0, NODES)
+    upper = apply(head, 0, 256)
+    lower = apply(tail, BACK, NODES)
+    rest = [
+        jnp.concatenate([upper[j * HEAD : (j + 1) * HEAD], lower[j * TAIL : (j + 1) * TAIL]], axis=0)
+        for j in range(2)
+    ]
+    return [first, *rest]
+
+
+def element_terms(grads, spacing, live, contract):
     slots = spacing.shape[1]
-    field_high, field_low = split(fields)
-    grads = (
-        jnp.dot(high, field_high, preferred_element_type=F32)
-        + jnp.dot(low, field_high, preferred_element_type=F32)
-        + jnp.dot(high, field_low, preferred_element_type=F32)
-    )
 
     def grad(field, i, j):
         column = (3 * field + i) * slots
-        return grads[j * ROWS : (j + 1) * ROWS, column : column + slots]
+        return grads[j][:, column : column + slots]
 
     def product(c, j):
         return sum(grad(0, i, c) * grad(1, i, j) for i in range(3))
@@ -134,41 +142,30 @@
     return (terms, jnp.where(live, spent, 0.0))
 
 
-def assemble(terms, target, blocks):
-    upper = quotient(target, LOW)
-    lower = remainder(target, LOW)
-    slots = target.shape[1]
-    rows = blocks * (ND_DEV // LOW)
-    row_index = lax.broadcasted_iota(jnp.int32, (rows, slots), 0)
-    low_index = lax.broadcasted_iota(jnp.int32, (LOW, slots), 0)
-    parts = []
-    for term in terms:
-        high = term.astype(BF16).astype(F32)
-        parts.append(high)
-    for c in range(3):
-        parts.append(terms[c] - parts[c])
-    left = []
-    right = []
+def place(index, rows, values=None):
+    slots = index.shape[1]
+    row = lax.broadcasted_iota(jnp.int32, (rows, slots), 0)
+    columns = []
     for k in range(8):
-        hit = row_index == upper[k : k + 1]
-        left.append(
-            jnp.concatenate([jnp.where(hit, p[k : k + 1], 0.0).astype(BF16) for p in parts], axis=0)
-        )
-        right.append(jnp.where(low_index == lower[k : k + 1], 1.0, 0.0).astype(BF16))
-    sums = lax.dot_general(
-        jnp.concatenate(left, axis=1),
-        jnp.concatenate(right, axis=1),
-        (((1,), (1,)), ((), ())),
-        preferred_element_type=F32,
-    )
-    return [sums[c * rows : (c + 1) * rows] + sums[(3 + c) * rows : (4 + c) * rows] for c in range(3)]
+        hit = row == index[k : k + 1]
+        if values is None:
+            columns.append(jnp.where(hit, 1.0, 0.0).astype(BF16))
+        else:
+            columns.append(
+                jnp.concatenate(
+                    [jnp.where(hit, v[k : k + 1], 0.0).astype(BF16) for v in values], axis=0
+                )
+            )
+    return jnp.concatenate(columns, axis=1)
 
 
 def kernel(
     groups, columns,
-    velocity, adjoint, spacing, count, design_map, high, low, contract,
+    velocity_in, adjoint_in, spacing_in, count_in, map_in, far_in, head_in, tail_in, contract_in,
     direction, objective,
-    outgoing, arrived, gathered, send_sem, recv_sem, send_all, recv_all,
+    velocity, adjoint, spacing, count, design_map, far, head, tail, contract,
+    outgoing, maps, arrived, placed, gathered,
+    local_sem, send_map, recv_map, send_sem, recv_sem, send_all, recv_all,
 ):
     devices = groups * columns
     grp, col = lax.axis_index("grp"), lax.axis_index("elem")
@@ -176,6 +173,14 @@
     slots = spacing.shape[1]
 
     barrier = pltpu.get_barrier_semaphore()
+    pairs = [
+        (head_in, head), (velocity_in, velocity), (adjoint_in, adjoint), (far_in, far),
+        (tail_in, tail), (map_in, design_map), (spacing_in, spacing), (count_in, count),
+        (contract_in, contract),
+    ]
+    loads = [pltpu.make_async_copy(a, b, local_sem.at[i]) for i, (a, b) in enumerate(pairs)]
+    for load in loads:
+        load.start()
 
     def coords(step):
         peer = lax.rem(me + step, devices)
@@ -186,46 +191,73 @@
         return carry
 
     lax.fori_loop(1, devices, greet, 0)
-
-    live = lax.broadcasted_iota(jnp.int32, (8, slots), 1) < count[0]
+    for load in loads:
+        load.wait()
+
     fields = jnp.concatenate([f[i] for f in (velocity, adjoint) for i in range(3)], axis=1)
-    terms, spent = element_terms(fields, spacing[...], live, high[...], low[...], contract[...])
-    node = design_map[...]
-    owner = quotient(node, ND_DEV)
-    offset = remainder(remainder(owner, columns) - col + (1 + columns), columns)
-    block = offset * groups + quotient(owner, columns)
-    sums = assemble(terms, block * ND_DEV + remainder(node, ND_DEV), 3 * groups)
-    for b in range(3 * groups):
-        for c in range(3):
-            outgoing[b, 8 * c : 8 * c + 8, :] = sums[c][8 * b : 8 * b + 8]
+    grads = derivatives(fields, far[...], head[...], tail[...])
 
     pl.semaphore_wait(barrier, devices - 1)
-
-    copies = []
+    own = groups
+    partners = []
     for step in [*range(groups // 2, groups), *range(groups // 2)]:
         for o in range(3):
-            if step == 0 and o == 1:
-                continue
-            to_grp = lax.rem(grp + step, groups)
             slot = o * groups + step
-            copy = pltpu.make_async_remote_copy(
-                src_ref=outgoing.at[o * groups + to_grp],
-                dst_ref=arrived.at[slot],
-                send_sem=send_sem.at[slot],
-                recv_sem=recv_sem.at[slot],
-                device_id=(to_grp, lax.rem(col + (o - 1 + columns), columns)),
+            if slot != own:
+                there = (lax.rem(grp + step, groups), lax.rem(col + (o - 1 + columns), columns))
+                partners.append((slot, there))
+
+    def copies(source, target, send, receive):
+        return {
+            slot: pltpu.make_async_remote_copy(
+                src_ref=source,
+                dst_ref=target.at[slot],
+                send_sem=send.at[slot],
+                recv_sem=receive.at[slot],
+                device_id=there,
                 device_id_type=MESH,
             )
-            copy.start()
-            copies.append((slot, copy))
-    total = outgoing[groups + grp]
-    for slot, copy in copies[::-1]:
+            for slot, there in partners
+        }
+
+    map_copies = copies(design_map, maps, send_map, recv_map)
+    for copy in map_copies.values():
+        copy.start()
+
+    live = lax.broadcasted_iota(jnp.int32, (8, slots), 1) < count[0]
+    terms, spent = element_terms(grads, spacing[...], live, contract[...])
+    for c in range(3):
+        outgoing[8 * c : 8 * c + 8, :] = terms[c]
+    term_copies = copies(outgoing, arrived, send_sem, recv_sem)
+    for copy in term_copies.values():
+        copy.start()
+
+    for slot, copy in map_copies.items():
+        copy.wait()
+        placed[slot] = place(maps[slot] & (LANES - 1), LANES)
+
+    base = me * UPPER
+
+    def collect(nodes, term, lower):
+        index = lax.shift_right_logical(nodes, jnp.full_like(nodes, LANES.bit_length() - 1)) - base
+        highs = [term[8 * c : 8 * c + 8].astype(BF16).astype(F32) for c in range(3)]
+        lows = [term[8 * c : 8 * c + 8] - highs[c] for c in range(3)]
+        return lax.dot_general(
+            place(index, UPPER, highs + lows),
+            lower,
+            (((1,), (1,)), ((), ())),
+            preferred_element_type=F32,
+        )
+
+    nodes = design_map[...]
+    both = collect(nodes, outgoing[...], place(nodes & (LANES - 1), LANES))
+    for slot, copy in list(term_copies.items())[::-1]:
         copy.wait_recv()
-        total = total + arrived[slot]
+        both = both + collect(maps[slot], arrived[slot], placed[slot])
+    total = both[: 3 * UPPER] + both[3 * UPPER :]
 
     squares = total * total
-    squares = squares[0:8] + squares[8:16] + squares[16:24]
-    squares = squares[:, :LANES] + squares[:, LANES:]
+    squares = sum(squares[8 * i : 8 * i + 8] for i in range(3 * UPPER // 8))
     lane = lax.broadcasted_iota(jnp.int32, (8, LANES), 1)
     mixed = jnp.where(
         lane < LANES // 2,
@@ -257,7 +289,7 @@
         return carry
 
     lax.fori_loop(1, devices, send, 0)
-    for slot, copy in copies:
+    for copy in term_copies.values():
         copy.wait_send()
     lax.fori_loop(1, devices, receive, 0)
     everything = jnp.sum(gathered[...], axis=0)
@@ -267,7 +299,7 @@
     scale = lax.rsqrt(square_total * (1.0 / (3.0 * ND_DEV * devices)) + 1e-06)
     scaled = total * scale
     for c in range(3):
-        direction[c] = scaled[8 * c : 8 * c + 8]
+        direction[c] = scaled[UPPER * c : UPPER * c + UPPER]
     objective[...] = spent_total * (1.0 / (NODES * slots * devices))
     lax.fori_loop(1, devices, finish, 0)
 
@@ -275,26 +307,35 @@
 def body(groups, columns, velocity, adjoint, spacing, elem_count, design_map):
     devices = groups * columns
     blocks = 3 * groups
+    slots = spacing.shape[1]
     vmem = pl.BlockSpec(memory_space=pltpu.VMEM)
+    constants = tables()
     direction, objective = pl.pallas_call(
         functools.partial(kernel, groups, columns),
         out_shape=(
-            jax.ShapeDtypeStruct((3, ND_DEV // LOW, LOW), F32),
+            jax.ShapeDtypeStruct((3, UPPER, LANES), F32),
             jax.ShapeDtypeStruct((1, 1), F32),
         ),
-        in_specs=[vmem, vmem, vmem, pl.BlockSpec(memory_space=pltpu.SMEM), vmem, vmem, vmem, vmem],
+        in_specs=[pl.BlockSpec(memory_space=pl.ANY)] * 9,
         out_specs=(vmem, vmem),
         scratch_shapes=[
-            pltpu.VMEM((blocks, 24, LOW), F32),
-            pltpu.VMEM((blocks, 24, LOW), F32),
+            pltpu.VMEM(velocity.shape, F32),
+            pltpu.VMEM(adjoint.shape, F32),
+            pltpu.VMEM(spacing.shape, F32),
+            pltpu.SMEM((1,), jnp.int32),
+            pltpu.VMEM((8, slots), jnp.int32),
+            *[pltpu.VMEM(table.shape, BF16) for table in constants],
+            pltpu.VMEM((24, slots), F32),
+            pltpu.VMEM((blocks, 8, slots), jnp.int32),
+            pltpu.VMEM((blocks, 24, slots), F32),
+            pltpu.VMEM((blocks, LANES, 8 * slots), BF16),
             pltpu.VMEM((devices, 1, LANES), F32),
-            pltpu.SemaphoreType.DMA((blocks,)),
-            pltpu.SemaphoreType.DMA((blocks,)),
-            pltpu.SemaphoreType.DMA((devices,)),
-            pltpu.SemaphoreType.DMA((devices,)),
+            pltpu.SemaphoreType.DMA((9,)),
+            *[pltpu.SemaphoreType.DMA((blocks,))] * 4,
+            *[pltpu.SemaphoreType.DMA((devices,))] * 2,
         ],
         compiler_params=pltpu.CompilerParams(collective_id=0, has_side_effects=True),
-    )(velocity, adjoint, spacing, elem_count, design_map, *tables())
+    )(velocity, adjoint, spacing, elem_count, design_map, *constants)
     return (direction.reshape(3, ND_DEV), objective.reshape(()))
 
 

time: 28 us -> 26.1 us (0.932)
  Pallas kernels: 23.3 us -> 21.4 us
    pallas_call x1, Pallas kernels: 23.3 us -> 21.4 us  [body(): pl.pallas_call(functools.partial(kernel, groups, columns), out_shape=(jax...]
where the time goes in v2:
time: 26.1 us; the launch traced here: 25.8 us
  Pallas kernels  21.4 us (82%)
  between operations  3.05 us (12%)
  local copies, waits for them, and re-layouts  1.37 us (5%)
    pallas_call x1, Pallas kernels, body(): pl.pallas_call(functools.partial(kernel, groups, columns), out_shape=(jax...  21.4 us
    unnamed x1, local copies, waits for them, and re-layouts  1.37 us

profile of v2, /device:TPU:0, one launch (start us, length us, event | category | flops | bytes accessed | tf_op | source)
XLA Modules:
  0.0 25.8 jit_solution(12291780824260301811)
XLA Ops:
  1.3 21.4 %shard_map.104 = (f32[3,16,128]{2,1,0:T(8,128)}, f32[1,1]{1,0:T(1,128)}) custom-call(f32[3,343,128]{2,1,0:T(8,128)} %velocity_in.1, f32[3,343,128]{2,1,0:T(8,128)} %adjoint_in.1, f32[3,128]{1,0:T(4,128)} %spacing_in.1, s32[1]{0:T(128)S(6)} %copy.15.count_in, s32[8,128]{1,0:T(8,128)} %map_in.1, bf16[2,352,343]{2,1,0:T(8,128)(2,1)} %constant.8.clone.far_in, ...), custom_call_target="tpu_custom_call" | custom-call | tf_op jit(solution)/shard_map/pallas_call | solution.py:313
  22.7 1.4 %copy.13 = f32[1,3,16,128]{3,1,2,0:T(4,128)} copy(f32[1,3,16,128]{3,2,1,0:T(8,128)} %bitcast.6) | data formatting | bytes 49152

commit v3 on v2

--- a/solution.py
+++ b/solution.py
@@ -44,10 +44,9 @@
     return (high, low)
 
 
-def tables():
+def derivative_table():
     degree = P_SIZE - 1
     points, values = lobatto(degree)
-    weights = 2.0 / (degree * (degree + 1) * values**2)
     derivative = np.zeros((P_SIZE, P_SIZE))
     for i in range(P_SIZE):
         for j in range(P_SIZE):
@@ -55,6 +54,14 @@
                 derivative[i, j] = values[i] / (values[j] * (points[i] - points[j]))
     derivative[0, 0] = -degree * (degree + 1) / 4.0
     derivative[P_SIZE - 1, P_SIZE - 1] = degree * (degree + 1) / 4.0
+    return derivative
+
+
+def tables():
+    degree = P_SIZE - 1
+    points, values = lobatto(degree)
+    weights = 2.0 / (degree * (degree + 1) * values**2)
+    derivative = derivative_table()
     coords = np.meshgrid(points, points, points, indexing="ij")
     coords = [c.reshape(-1) for c in coords]
     spread = np.meshgrid(weights, weights, weights, indexing="ij")
@@ -68,13 +75,10 @@
             contract[8 * j + vertex, :NODES] = signs[j] / 2.0 * others[0] * others[1] * quadrature
     contract[24, :NODES] = quadrature
     unit = np.eye(P_SIZE)
-    directional = np.zeros((3, ROWS, NODES))
-    directional[0, :NODES] = np.kron(np.kron(derivative, unit), unit)
-    directional[1, :NODES] = np.kron(np.kron(unit, derivative), unit)
-    directional[2, :NODES] = np.kron(np.kron(unit, unit), derivative)
-    near = directional[1:]
+    near = np.zeros((2, ROWS, NODES))
+    near[0, :NODES] = np.kron(np.kron(unit, derivative), unit)
+    near[1, :NODES] = np.kron(np.kron(unit, unit), derivative)
     return (
-        np.stack(halves(directional[0])),
         np.stack(halves(near[:, :HEAD, :256].reshape(2 * HEAD, 256))),
         np.stack(halves(near[:, HEAD:, BACK:].reshape(2 * TAIL, NODES - BACK))),
         np.concatenate(halves(contract)),
@@ -86,7 +90,20 @@
     return (high, (value - high.astype(F32)).astype(BF16))
 
 
-def derivatives(fields, far, head, tail):
+def far_derivatives(velocity, adjoint, far):
+    table = derivative_table()
+    width = P_SIZE * P_SIZE
+    for f, field in enumerate((velocity, adjoint)):
+        for i in range(3):
+            far[3 * f + i, ROWS - 16 :, :] = jnp.zeros((16, field.shape[2]), F32)
+            slabs = [field[i, pl.ds(width * a, width), :] for a in range(P_SIZE)]
+            for a in range(P_SIZE):
+                far[3 * f + i, pl.ds(width * a, width), :] = sum(
+                    float(table[a, b]) * slabs[b] for b in range(P_SIZE)
+                )
+
+
+def near_derivatives(fields, head, tail):
     high, low = split(fields)
 
     def apply(table, begin, end):
@@ -96,22 +113,20 @@
             + jnp.dot(table[0], low[begin:end], preferred_element_type=F32)
         )
 
-    first = apply(far, 0, NODES)
     upper = apply(head, 0, 256)
     lower = apply(tail, BACK, NODES)
-    rest = [
+    return [
         jnp.concatenate([upper[j * HEAD : (j + 1) * HEAD], lower[j * TAIL : (j + 1) * TAIL]], axis=0)
         for j in range(2)
     ]
-    return [first, *rest]
-
-
-def element_terms(grads, spacing, live, contract):
+
+
+def element_terms(far, near, spacing, live, contract):
     slots = spacing.shape[1]
 
     def grad(field, i, j):
         column = (3 * field + i) * slots
-        return grads[j][:, column : column + slots]
+        return near[j - 1][:, column : column + slots] if j else far[3 * field + i]
 
     def product(c, j):
         return sum(grad(0, i, c) * grad(1, i, j) for i in range(3))
@@ -161,9 +176,9 @@
 
 def kernel(
     groups, columns,
-    velocity_in, adjoint_in, spacing_in, count_in, map_in, far_in, head_in, tail_in, contract_in,
+    velocity_in, adjoint_in, spacing_in, count_in, map_in, head_in, tail_in, contract_in,
     direction, objective,
-    velocity, adjoint, spacing, count, design_map, far, head, tail, contract,
+    velocity, adjoint, spacing, count, design_map, head, tail, contract, far,
     outgoing, maps, arrived, placed, gathered,
     local_sem, send_map, recv_map, send_sem, recv_sem, send_all, recv_all,
 ):
@@ -174,9 +189,8 @@
 
     barrier = pltpu.get_barrier_semaphore()
     pairs = [
-        (head_in, head), (velocity_in, velocity), (adjoint_in, adjoint), (far_in, far),
-        (tail_in, tail), (map_in, design_map), (spacing_in, spacing), (count_in, count),
-        (contract_in, contract),
+        (velocity_in, velocity), (adjoint_in, adjoint), (head_in, head), (tail_in, tail),
+        (map_in, design_map), (spacing_in, spacing), (count_in, count), (contract_in, contract),
     ]
     loads = [pltpu.make_async_copy(a, b, local_sem.at[i]) for i, (a, b) in enumerate(pairs)]
     for load in loads:
@@ -191,12 +205,15 @@
         return carry
 
     lax.fori_loop(1, devices, greet, 0)
-    for load in loads:
+    for load in loads[:4]:
         load.wait()
 
     fields = jnp.concatenate([f[i] for f in (velocity, adjoint) for i in range(3)], axis=1)
-    grads = derivatives(fields, far[...], head[...], tail[...])
-
+    near = near_derivatives(fields, head, tail)
+    far_derivatives(velocity, adjoint, far)
+
+    for load in loads[4:]:
+        load.wait()
     pl.semaphore_wait(barrier, devices - 1)
     own = groups
     partners = []
@@ -225,16 +242,12 @@
         copy.start()
 
     live = lax.broadcasted_iota(jnp.int32, (8, slots), 1) < count[0]
-    terms, spent = element_terms(grads, spacing[...], live, contract[...])
+    terms, spent = element_terms(far, near, spacing[...], live, contract[...])
     for c in range(3):
         outgoing[8 * c : 8 * c + 8, :] = terms[c]
     term_copies = copies(outgoing, arrived, send_sem, recv_sem)
     for copy in term_copies.values():
         copy.start()
-
-    for slot, copy in map_copies.items():
-        copy.wait()
-        placed[slot] = place(maps[slot] & (LANES - 1), LANES)
 
     base = me * UPPER
 
@@ -251,6 +264,10 @@
 
     nodes = design_map[...]
     both = collect(nodes, outgoing[...], place(nodes & (LANES - 1), LANES))
+    for slot, copy in map_copies.items():
+        copy.wait()
+        placed[slot] = place(maps[slot] & (LANES - 1), LANES)
+
     for slot, copy in list(term_copies.items())[::-1]:
         copy.wait_recv()
         both = both + collect(maps[slot], arrived[slot], placed[slot])
@@ -316,7 +333,7 @@
             jax.ShapeDtypeStruct((3, UPPER, LANES), F32),
             jax.ShapeDtypeStruct((1, 1), F32),
         ),
-        in_specs=[pl.BlockSpec(memory_space=pl.ANY)] * 9,
+        in_specs=[pl.BlockSpec(memory_space=pl.ANY)] * 8,
         out_specs=(vmem, vmem),
         scratch_shapes=[
             pltpu.VMEM(velocity.shape, F32),
@@ -325,12 +342,13 @@
             pltpu.SMEM((1,), jnp.int32),
             pltpu.VMEM((8, slots), jnp.int32),
             *[pltpu.VMEM(table.shape, BF16) for table in constants],
+            pltpu.VMEM((6, ROWS, slots), F32),
             pltpu.VMEM((24, slots), F32),
             pltpu.VMEM((blocks, 8, slots), jnp.int32),
             pltpu.VMEM((blocks, 24, slots), F32),
             pltpu.VMEM((blocks, LANES, 8 * slots), BF16),
             pltpu.VMEM((devices, 1, LANES), F32),
-            pltpu.SemaphoreType.DMA((9,)),
+            pltpu.SemaphoreType.DMA((8,)),
             *[pltpu.SemaphoreType.DMA((blocks,))] * 4,
             *[pltpu.SemaphoreType.DMA((devices,))] * 2,
         ],

time: 26.1 us -> 25.8 us (0.989)
  no operation moved by 1% of the time
where the time goes in v3:
time: 25.8 us; the launch traced here: 25.6 us
  Pallas kernels  21.2 us (82%)
  between operations  3.05 us (12%)
  local copies, waits for them, and re-layouts  1.37 us (5%)
    pallas_call x1, Pallas kernels, body(): pl.pallas_call(functools.partial(kernel, groups, columns), out_shape=(jax...  21.2 us
    unnamed x1, local copies, waits for them, and re-layouts  1.37 us

profile of v3, /device:TPU:0, one launch (start us, length us, event | category | flops | bytes accessed | tf_op | source)
XLA Modules:
  0.0 25.6 jit_solution(2626034407970317586)
XLA Ops:
  1.3 21.2 %shard_map.95 = (f32[3,16,128]{2,1,0:T(8,128)}, f32[1,1]{1,0:T(1,128)}) custom-call(f32[3,343,128]{2,1,0:T(8,128)} %velocity_in.1, f32[3,343,128]{2,1,0:T(8,128)} %adjoint_in.1, f32[3,128]{1,0:T(4,128)} %spacing_in.1, s32[1]{0:T(128)S(6)} %copy.14.count_in, s32[8,128]{1,0:T(8,128)} %map_in.1, bf16[2,480,256]{2,1,0:T(8,128)(2,1)} %constant.6.clone.head_in, ...), custom_call_target="tpu_custom_call" | custom-call | tf_op jit(solution)/shard_map/pallas_call | solution.py:330
  22.5 1.4 %copy.12 = f32[1,3,16,128]{3,1,2,0:T(4,128)} copy(f32[1,3,16,128]{3,2,1,0:T(8,128)} %bitcast.6) | data formatting | bytes 49152

commit v4 on v3

--- a/solution.py
+++ b/solution.py
@@ -214,7 +214,6 @@
 
     for load in loads[4:]:
         load.wait()
-    pl.semaphore_wait(barrier, devices - 1)
     own = groups
     partners = []
     for step in [*range(groups // 2, groups), *range(groups // 2)]:
@@ -238,14 +237,15 @@
         }
 
     map_copies = copies(design_map, maps, send_map, recv_map)
-    for copy in map_copies.values():
-        copy.start()
 
     live = lax.broadcasted_iota(jnp.int32, (8, slots), 1) < count[0]
     terms, spent = element_terms(far, near, spacing[...], live, contract[...])
     for c in range(3):
         outgoing[8 * c : 8 * c + 8, :] = terms[c]
     term_copies = copies(outgoing, arrived, send_sem, recv_sem)
+    pl.semaphore_wait(barrier, devices - 1)
+    for copy in map_copies.values():
+        copy.start()
     for copy in term_copies.values():
         copy.start()
 

time: 25.8 us -> 25.9 us (level)
  no operation moved by 1% of the time
where the time goes in v4:
time: 25.9 us; the launch traced here: 25.6 us
  Pallas kernels  21.2 us (82%)
  between operations  3.05 us (12%)
  local copies, waits for them, and re-layouts  1.37 us (5%)
    pallas_call x1, Pallas kernels, body(): pl.pallas_call(functools.partial(kernel, groups, columns), out_shape=(jax...  21.2 us
    unnamed x1, local copies, waits for them, and re-layouts  1.37 us

profile of v4, /device:TPU:0, one launch (start us, length us, event | category | flops | bytes accessed | tf_op | source)
XLA Modules:
  0.0 25.6 jit_solution(8604408763790388391)
XLA Ops:
  1.3 21.2 %shard_map.95 = (f32[3,16,128]{2,1,0:T(8,128)}, f32[1,1]{1,0:T(1,128)}) custom-call(f32[3,343,128]{2,1,0:T(8,128)} %velocity_in.1, f32[3,343,128]{2,1,0:T(8,128)} %adjoint_in.1, f32[3,128]{1,0:T(4,128)} %spacing_in.1, s32[1]{0:T(128)S(6)} %copy.14.count_in, s32[8,128]{1,0:T(8,128)} %map_in.1, bf16[2,480,256]{2,1,0:T(8,128)(2,1)} %constant.6.clone.head_in, ...), custom_call_target="tpu_custom_call" | custom-call | tf_op jit(solution)/shard_map/pallas_call | solution.py:330
  22.5 1.4 %copy.12 = f32[1,3,16,128]{3,1,2,0:T(4,128)} copy(f32[1,3,16,128]{3,2,1,0:T(8,128)} %bitcast.6) | data formatting | bytes 49152
